TPU v7x, 32 devices: a whole 2x2x4 slice. The times are simulated.
32 devices in a mesh: dp: 8 (over y, x, core), fsdp: 4 (over z).
Axes of the slice: x: 2, y: 2, z: 4, core: 2. Of those that a mesh axis runs over, the one named last changes fastest.
Arguments:
- tokens: bfloat16 [64, 512, 768], P(('dp', 'fsdp')), may hold values from -6 to 6
- lengths: int32 [64], P(('dp', 'fsdp')), may hold values from 1 to 512, 24576 in all
- cotangent: bfloat16 [64, 512, 768], P(('dp', 'fsdp')), may hold values from -6 to 6
- w_query: bfloat16 [768, 768], P(('dp', 'fsdp')), may hold values from -0.21875 to 0.21875
- w_key: bfloat16 [768, 768], P(('dp', 'fsdp')), may hold values from -0.21875 to 0.21875
- w_value: bfloat16 [768, 768], P(('dp', 'fsdp')), may hold values from -0.21875 to 0.21875
- w_out: bfloat16 [768, 768], P(('dp', 'fsdp')), may hold values from -0.875 to 0.875
- w_up: bfloat16 [768, 3072], P(('dp', 'fsdp')), may hold values from -0.21875 to 0.21875
- w_down: bfloat16 [3072, 768], P(('dp', 'fsdp')), may hold values from -0.109375 to 0.109375
- shared_a: bfloat16 [768, 1024], P(('dp', 'fsdp')), may hold values from -0.21875 to 0.21875
- shared_b: bfloat16 [1024, 768], P(('dp', 'fsdp')), may hold values from -0.1875 to 0.1875
- gain_one: float32 [768], replicated, may hold values from 0.5 to 1.5
- gain_two: float32 [768], replicated, may hold values from 0.5 to 1.5
- query_d: float32 [1024], replicated, may hold values from -4 to 4
- query_b: float32 [768], replicated, may hold values from -4 to 4
- value_d: float32 [1024], replicated, may hold values from -4 to 4
- value_b: float32 [768], replicated, may hold values from -4 to 4
Outputs:
- output: bfloat16 [64, 512, 768], P(('dp', 'fsdp'))
- grad_tokens: bfloat16 [64, 512, 768], P(('dp', 'fsdp'))
- grad_query_d: float32 [1024], replicated
- grad_query_b: float32 [768], replicated
- grad_value_d: float32 [1024], replicated
- grad_value_b: float32 [768], replicated
- rank_stats: float32 [1024], replicated
Inputs may be any that keep to these rules, and one draw needn't show every extreme that they name: The 64 lengths sum to 24576, and the largest equals 512.
All inputs are finite; a program needn't handle non-finite values. No bound on the sum of `lengths` on one device may be relied on, other than what follows from the above.
Results may differ from a plain program's by a relative error of at most 0.015.
The roundings to bfloat16 on the way count: a program that leaves them out, or rounds other values in their place, can miss the bound.
Values may be sent and summed in bfloat16 or wider, within the bound.
A program may use at most 192 MiB of HBM per device.

v0:
```python
import jax
import jax.numpy as jnp
from jax import lax
from jax.sharding import PartitionSpec as P

D = 768
H = 12
HD = 64
L = 512
SEQ_DEV = 2
eps_norm = 1e-05
neg_fill = -1000000000.0


def layer_norm(hidden, gain):
    center = jnp.mean(hidden, axis=-1, keepdims=True)
    shifted = hidden - center
    spread = jnp.mean(shifted * shifted, axis=-1, keepdims=True)
    return shifted * lax.rsqrt(spread + eps_norm) * gain


def exact_gelu(pre_act):
    return jax.nn.gelu(pre_act, approximate=False)


def dot_plain(left, right):
    return jnp.dot(left, right, preferred_element_type=jnp.float32)


def dot_trans(left, right):
    return lax.dot_general(
        left, right, (((1,), (1,)), ((), ())), preferred_element_type=jnp.float32
    )


def split_heads(row_data):
    return row_data.reshape(SEQ_DEV, L, H, HD).transpose(0, 2, 1, 3).reshape(SEQ_DEV * H, L, HD)


def join_heads(head_data):
    return head_data.reshape(SEQ_DEV, H, L, HD).transpose(0, 2, 1, 3).reshape(SEQ_DEV * L, D)


def shards(
    tokens,
    lengths,
    cotangent,
    w_query,
    w_key,
    w_value,
    w_out,
    w_up,
    w_down,
    shared_a,
    shared_b,
    gain_one,
    gain_two,
    query_d,
    query_b,
    value_d,
    value_b,
):
    row_count = SEQ_DEV * L
    head_scale = HD ** (-0.5)
    local_mats = (w_query, w_key, w_value, w_out, w_up, w_down, shared_a, shared_b)
    full_mats = (
        lax.all_gather(local_mats[0], ("dp", "fsdp"), axis=0, tiled=True),
        lax.all_gather(local_mats[1], ("dp", "fsdp"), axis=0, tiled=True),
        lax.all_gather(local_mats[2], ("dp", "fsdp"), axis=0, tiled=True),
        lax.all_gather(local_mats[3], ("dp", "fsdp"), axis=0, tiled=True),
        lax.all_gather(local_mats[4], ("dp", "fsdp"), axis=0, tiled=True),
        lax.all_gather(local_mats[5], ("dp", "fsdp"), axis=0, tiled=True),
        lax.all_gather(local_mats[6], ("dp", "fsdp"), axis=0, tiled=True),
        lax.all_gather(local_mats[7], ("dp", "fsdp"), axis=0, tiled=True),
    )
    wq, wk, wv, wo, wu, wd, mat_a, mat_b = full_mats
    inputs = tokens.reshape(row_count, D)
    positions = lax.broadcasted_iota(jnp.int32, (SEQ_DEV, L), 1)
    live = (positions < lengths[:, None]).astype(jnp.float32)
    live_rows = live.reshape(row_count, 1)
    key_live = jnp.repeat(live, H, axis=0)
    rank_act = dot_plain(inputs, mat_a)
    square_sum = jnp.sum(rank_act * rank_act * live_rows, axis=0)
    count = jnp.sum(lengths).astype(jnp.float32)
    total_square, total_count = lax.psum((square_sum, count), ("dp", "fsdp"))
    rank_q = (rank_act * query_d).astype(jnp.bfloat16)
    rank_v = (rank_act * value_d).astype(jnp.bfloat16)
    delta_q = dot_plain(rank_q, mat_b)
    delta_v = dot_plain(rank_v, mat_b)
    queries = (dot_plain(inputs, wq) + query_b * delta_q).astype(jnp.bfloat16)
    key_rows = dot_plain(inputs, wk).astype(jnp.bfloat16)
    values = (dot_plain(inputs, wv) + value_b * delta_v).astype(jnp.bfloat16)
    q_heads = split_heads(queries)
    k_heads = split_heads(key_rows)
    v_heads = split_heads(values)

    def attend_block(pieces):
        q_blk, k_blk, v_blk, live_keys = pieces
        scores = (
            jnp.einsum("qd,kd->qk", q_blk, k_blk, preferred_element_type=jnp.float32) * head_scale
        )
        scores = jnp.where(live_keys[None, :] > 0, scores, neg_fill)
        row_max = jnp.max(scores, axis=-1, keepdims=True)
        log_total = row_max + jnp.log(jnp.sum(jnp.exp(scores - row_max), axis=-1, keepdims=True))
        probs = jnp.exp(scores - log_total).astype(jnp.bfloat16)
        context = jnp.dot(probs, v_blk, preferred_element_type=jnp.float32).astype(jnp.bfloat16)
        return (context, log_total[:, 0])

    ctx_heads, log_totals = lax.map(attend_block, (q_heads, k_heads, v_heads, key_live))
    context = join_heads(ctx_heads)
    h_one = inputs + dot_plain(context, wo)
    x_one = layer_norm(h_one, gain_one)
    x_low = x_one.astype(jnp.bfloat16)

    def feed_block(block):
        act = exact_gelu(dot_plain(block, wu)).astype(jnp.bfloat16)
        return dot_plain(act, wd)

    x_blocks = x_low.reshape(SEQ_DEV, L, D)
    ffn_out = lax.map(feed_block, x_blocks).reshape(row_count, D)
    h_two = x_one + ffn_out
    output = layer_norm(h_two, gain_two)
    cot_rows = cotangent.reshape(row_count, D).astype(jnp.float32) * live_rows
    _, norm_two_back = jax.vjp(lambda hidden: layer_norm(hidden, gain_two), h_two)
    g_h2 = norm_two_back(cot_rows)[0]
    back_mats = (
        lax.all_gather(local_mats[0], ("dp", "fsdp"), axis=0, tiled=True),
        lax.all_gather(local_mats[1], ("dp", "fsdp"), axis=0, tiled=True),
        lax.all_gather(local_mats[2], ("dp", "fsdp"), axis=0, tiled=True),
        lax.all_gather(local_mats[3], ("dp", "fsdp"), axis=0, tiled=True),
        lax.all_gather(local_mats[4], ("dp", "fsdp"), axis=0, tiled=True),
        lax.all_gather(local_mats[5], ("dp", "fsdp"), axis=0, tiled=True),
        lax.all_gather(local_mats[6], ("dp", "fsdp"), axis=0, tiled=True),
        lax.all_gather(local_mats[7], ("dp", "fsdp"), axis=0, tiled=True),
    )
    bq_mat, bk_mat, bv_mat, bo_mat, bu_mat, bd_mat, back_a, back_b = back_mats
    g_ffn = g_h2.astype(jnp.bfloat16)

    def feed_back(pieces):
        block, grad_out = pieces
        pre_act = dot_plain(block, bu_mat)
        g_act = dot_trans(grad_out, bd_mat)
        _, gelu_back = jax.vjp(exact_gelu, pre_act)
        g_pre = gelu_back(g_act)[0].astype(jnp.bfloat16)
        return dot_trans(g_pre, bu_mat)

    g_x1 = g_h2 + lax.map(feed_back, (x_blocks, g_ffn.reshape(SEQ_DEV, L, D))).reshape(row_count, D)
    _, norm_one_back = jax.vjp(lambda hidden: layer_norm(hidden, gain_one), h_one)
    g_h1 = norm_one_back(g_x1)[0]
    g_attn = g_h1.astype(jnp.bfloat16)
    g_context = dot_trans(g_attn, bo_mat).astype(jnp.bfloat16)
    gc_heads = split_heads(g_context)

    def attend_back(pieces):
        q_blk, k_blk, v_blk, live_keys, log_total, gc_blk = pieces
        scores = (
            jnp.einsum("qd,kd->qk", q_blk, k_blk, preferred_element_type=jnp.float32) * head_scale
        )
        scores = jnp.where(live_keys[None, :] > 0, scores, neg_fill)
        probs = jnp.exp(scores - log_total[:, None])
        probs_low = probs.astype(jnp.bfloat16)
        g_probs = jnp.einsum("qd,kd->qk", gc_blk, v_blk, preferred_element_type=jnp.float32)
        g_scores = (probs * (g_probs - jnp.sum(g_probs * probs, axis=-1, keepdims=True))).astype(
            jnp.bfloat16
        )
        g_q = (jnp.dot(g_scores, k_blk, preferred_element_type=jnp.float32) * head_scale).astype(
            jnp.bfloat16
        )
        g_k = (
            jnp.einsum("qk,qd->kd", g_scores, q_blk, preferred_element_type=jnp.float32)
            * head_scale
        ).astype(jnp.bfloat16)
        g_v = jnp.einsum("qk,qd->kd", probs_low, gc_blk, preferred_element_type=jnp.float32).astype(
            jnp.bfloat16
        )
        return (g_q, g_k, g_v)

    gq_heads, gk_heads, gv_heads = lax.map(
        attend_back, (q_heads, k_heads, v_heads, key_live, log_totals, gc_heads)
    )
    g_queries = join_heads(gq_heads)
    g_keys = join_heads(gk_heads)
    g_values = join_heads(gv_heads)
    gq_wide = g_queries.astype(jnp.float32)
    gv_wide = g_values.astype(jnp.float32)
    grad_qb = jnp.sum(gq_wide * delta_q, axis=0)
    grad_vb = jnp.sum(gv_wide * delta_v, axis=0)
    g_dq = (query_b * gq_wide).astype(jnp.bfloat16)
    g_dv = (value_b * gv_wide).astype(jnp.bfloat16)
    t_q = dot_trans(g_dq, back_b)
    t_v = dot_trans(g_dv, back_b)
    grad_qd = jnp.sum(t_q * rank_act, axis=0)
    grad_vd = jnp.sum(t_v * rank_act, axis=0)
    g_rank = (t_q * query_d + t_v * value_d).astype(jnp.bfloat16)
    g_inputs = (
        g_h1
        + dot_trans(g_queries, bq_mat)
        + dot_trans(g_keys, bk_mat)
        + dot_trans(g_values, bv_mat)
        + dot_trans(g_rank, back_a)
    )
    sum_qd, sum_qb, sum_vd, sum_vb = lax.psum((grad_qd, grad_qb, grad_vd, grad_vb), ("dp", "fsdp"))
    rank_stats = total_square / total_count
    output_out = output.astype(jnp.bfloat16).reshape(SEQ_DEV, L, D)
    grad_tokens = g_inputs.astype(jnp.bfloat16).reshape(SEQ_DEV, L, D)
    return (output_out, grad_tokens, sum_qd, sum_qb, sum_vd, sum_vb, rank_stats)


def solution(mesh):
    in_specs = (
        P(("dp", "fsdp"), None, None),
        P(("dp", "fsdp")),
        P(("dp", "fsdp"), None, None),
        P(("dp", "fsdp"), None),
        P(("dp", "fsdp"), None),
        P(("dp", "fsdp"), None),
        P(("dp", "fsdp"), None),
        P(("dp", "fsdp"), None),
        P(("dp", "fsdp"), None),
        P(("dp", "fsdp"), None),
        P(("dp", "fsdp"), None),
        P(),
        P(),
        P(),
        P(),
        P(),
        P(),
    )
    out_specs = (
        P(("dp", "fsdp"), None, None),
        P(("dp", "fsdp"), None, None),
        P(),
        P(),
        P(),
        P(),
        P(),
    )
    return jax.shard_map(shards, mesh=mesh, in_specs=in_specs, out_specs=out_specs, check_vma=False)
```

profile of v0, /device:TPU:0, one launch (start us, length us, event | category | flops | bytes accessed | tf_op | source)
XLA Modules:
  0.0 919.7 jit_solution(1533905239916311515)
XLA Ops:
  15.9 51.6 %all-gather.15.cloned.1.call-done = bf16[768,768]{1,0:T(8,128)(2,1)} async-done(((bf16[24,768]{1,0:T(8,128)(2,1)}), bf16[768,768]{1,0:T(8,128)(2,1)}) %all-gather.15.cloned.1.call-update) | async-done | bytes 1179664 | tf_op jit(solution)/shard_map/all_gather | solution.py:68
  76.1 48.2 %all-gather.11.cloned.1.call-done = bf16[768,1024]{1,0:T(8,128)(2,1)} async-done(((bf16[24,1024]{1,0:T(8,128)(2,1)}), bf16[768,1024]{1,0:T(8,128)(2,1)}) %all-gather.11.cloned.1.call-update) | async-done | bytes 1572880 | tf_op jit(solution)/shard_map/all_gather | solution.py:73
  124.3 5.1 fusion.191
  129.5 51.7 %all-gather.13.cloned.1.call-done = bf16[1024,768]{1,0:T(8,128)(2,1)} async-done(((bf16[32,768]{1,0:T(8,128)(2,1)}), bf16[1024,768]{1,0:T(8,128)(2,1)}) %all-gather.13.cloned.1.call-update) | async-done | bytes 1572880 | tf_op jit(solution)/shard_map/all_gather | solution.py:74
  181.1 4.5 fusion.169
  185.6 51.1 %all-gather.9.cloned.1.call-done = bf16[768,768]{1,0:T(8,128)(2,1)} async-done(((bf16[24,768]{1,0:T(8,128)(2,1)}), bf16[768,768]{1,0:T(8,128)(2,1)}) %all-gather.9.cloned.1.call-update) | async-done | bytes 1179664 | tf_op jit(solution)/shard_map/all_gather | solution.py:67
  236.7 4.3 add_convert_fusion.3
  247.4 4.5 fusion.170
  251.9 40.4 %all-gather.17.cloned.1.call-done = bf16[768,768]{1,0:T(8,128)(2,1)} async-done(((bf16[24,768]{1,0:T(8,128)(2,1)}), bf16[768,768]{1,0:T(8,128)(2,1)}) %all-gather.17.cloned.1.call-update) | async-done | bytes 1179664 | tf_op jit(solution)/shard_map/all_gather | solution.py:69
  292.3 4.3 add_convert_fusion.2
  300.7 4.1 copy.63
  306.1 91.2 %while.46 = (s32[]{:T(128)}, bf16[24,512,64]{1,2,0:T(8,128)(2,1)}, f32[24,512]{1,0:T(8,128)}, f32[24,512]{1,0:T(8,128)S(1)}, bf16[24,512,64]{2,1,0:T(8,128)(2,1)...) while((s32[]{:T(128)}, bf16[24,512,64]{1,2,0:T(8,128)(2,1)}, ...), condition=%wide.region_3.0_spmd, body=%wide.region_0.3_spmd.sunk | while | flops 68976640 | bytes 3628133 | solution.py:109
  397.3 4.2 copy.49
  413.3 64.7 %all-gather.23.cloned.1.call-done = bf16[3072,768]{1,0:T(8,128)(2,1)} async-done(((bf16[96,768]{1,0:T(8,128)(2,1)}), bf16[3072,768]{1,0:T(8,128)(2,1)}) %all-gather.23.cloned.1.call-update) | async-done | bytes 4718608 | tf_op jit(solution)/shard_map/all_gather | solution.py:72
  479.9 44.2 %while.47 = (s32[]{:T(128)}, f32[2,512,768]{2,1,0:T(8,128)}, bf16[2,512,768]{2,1,0:T(8,128)(2,1)}, bf16[768,3072]{1,0:T(8,128)(2,1)}, bf16[3072,768]{1,0:T(8,128)(2,1)}, /*index=5*/s32[]{:T(128)}) while((s32[]{:T(128)}, f32[2,512,768]{2,1,0:T(8,128)}, bf16[2,512,768]{2,1,0:T(8,128)(2,1)}, bf16[768,3072]{1,0:T(8,128)(2,1)}, ...), condition=%wide.region_7.8_spmd, body=%wide.region_6.7_spmd.sunk | while | flops 4934074368 | bytes 11797573 | solution.py:120
  479.9 22.0 %bitcast_dynamic-update-slice_fusion.4 = f32[2,512,768]{2,1,0:T(8,128)} fusion(f32[2,512,768]{2,1,0:T(8,128)} %get-tuple-element.483, s32[]{:T(128)} %get-tuple-element.482, bf16[3072,768]{1,0:T(8,128)(2,1)} %get-tuple-element.492, bf16[768,3072]{1,0:T(8,128)(2,1)} %get-tuple-element.491, bf16[2,512,768]{2,1,0:T(8,128)(2,1)} %get-tuple-element.490), kind=kOutput, calls=%fused_computation.20.clone.1 | convolution fusion | flops 4934074368 | bytes 11797504 | tf_op jit(solution)/shard_map/while/body/eval_jaxpr/dot_general | solution.py:27
  501.9 21.8 %bitcast_dynamic-update-slice_fusion.4 = f32[2,512,768]{2,1,0:T(8,128)} fusion(f32[2,512,768]{2,1,0:T(8,128)} %get-tuple-element.483, s32[]{:T(128)} %get-tuple-element.482, bf16[3072,768]{1,0:T(8,128)(2,1)} %get-tuple-element.492, bf16[768,3072]{1,0:T(8,128)(2,1)} %get-tuple-element.491, bf16[2,512,768]{2,1,0:T(8,128)(2,1)} %get-tuple-element.490), kind=kOutput, calls=%fused_computation.20.clone.1 | convolution fusion | flops 4934074368 | bytes 11797504 | tf_op jit(solution)/shard_map/while/body/eval_jaxpr/dot_general | solution.py:27
  534.7 67.9 %while.48 = (s32[]{:T(128)}, f32[2,512,768]{2,1,0:T(8,128)}, bf16[2,512,768]{2,1,0:T(8,128)(2,1)}, bf16[768,3072]{1,0:T(8,128)(2,1)}, bf16[2,512,768]{2,1,0:T(8,128)(2,1)}, /*index=5*/bf16[3072,768]{1,0:T(8,128)(2,1)}, s32[]{:T(128)}) while((s32[]{:T(128)}, f32[2,512,768]{2,1,0:T(8,128)}, bf16[2,512,768]{2,1,0:T(8,128)(2,1)}, ...), condition=%wide.region_13.14_spmd, body=%wide.region_12.13_spmd.sunk | while | flops 7361003520 | bytes 29886028 | solution.py:147
  537.2 7.8 fusion.262
  545.1 24.7 %bitcast_dynamic-update-slice_fusion.5 = f32[2,512,768]{2,1,0:T(8,128)} fusion(f32[2,512,768]{2,1,0:T(8,128)} %get-tuple-element.502, s32[]{:T(128)} %get-tuple-element.501, bf16[768,3072]{1,0:T(8,128)(2,1)} %get-tuple-element.511, f32[512,3072]{1,0:T(8,128)} %fusion.262, bf16[3072,768]{1,0:T(8,128)(2,1)} %get-tuple-element.513, ...), kind=kOutput, calls=%fused_computation.77.clone.1 | convolution fusion | flops 4945084416 | bytes 18088960 | tf_op jit(solution)/shard_map/while/body/eval_jaxpr/dot_general | solution.py:31
  569.7 7.8 fusion.262
  577.6 24.6 %bitcast_dynamic-update-slice_fusion.5 = f32[2,512,768]{2,1,0:T(8,128)} fusion(f32[2,512,768]{2,1,0:T(8,128)} %get-tuple-element.502, s32[]{:T(128)} %get-tuple-element.501, bf16[768,3072]{1,0:T(8,128)(2,1)} %get-tuple-element.511, f32[512,3072]{1,0:T(8,128)} %fusion.262, bf16[3072,768]{1,0:T(8,128)(2,1)} %get-tuple-element.513, ...), kind=kOutput, calls=%fused_computation.77.clone.1 | convolution fusion | flops 4945084416 | bytes 18088960 | tf_op jit(solution)/shard_map/while/body/eval_jaxpr/dot_general | solution.py:31
  623.6 211.6 %while.49 = (s32[]{:T(128)}, bf16[24,512,64]{1,2,0:T(8,128)(2,1)}, bf16[24,512,64]{1,2,0:T(8,128)(2,1)}, bf16[24,512,64]{1,2,0:T(8,128)(2,1)}, f32[24,512]{1,0:T...) while((s32[]{:T(128)}, bf16[24,512,64]{1,2,0:T(8,128)(2,1)}, ...), condition=%wide.region_18.19_spmd, body=%wide.region_16.18_spmd.sunk | while | flops 170295296 | bytes 8996981 | solution.py:178
  858.3 39.8 %all-reduce = (f32[1024]{0:T(1024)}, f32[768]{0:T(1024)}, f32[1024]{0:T(1024)}, f32[768]{0:T(1024)}, f32[1024]{0:T(1024)S(1)}, /*index=5*/f32[]{:T(128)}) all-reduce(f32[1024]{0:T(1024)S(1)} %get-tuple-element.184, f32[768]{0:T(1024)S(1)} %get-tuple-element.267, ...), channel_id=1, replica_groups=mesh['dp'=8,'fsdp'=4] {'dp','fsdp'}, use_global_device_ids=true, to_apply=%region_20.21 | all-reduce | flops 4609 | bytes 36872 | tf_op jit(solution)/shard_map/psum | solution.py:202
  (512 shorter events, 412.7 us)
Async XLA Ops:
  7.2 60.3 %all-gather.15.cloned.1.call-start = ((), (), s32[]{:S(2)}) async-start(), calls=%async_computation.3 | async-start | bytes 1216512 | tf_op jit(solution)/shard_map/all_gather | solution.py:68
  7.9 116.4 %all-gather.11.cloned.1.call-start = ((), (), s32[]{:S(2)}) async-start(), calls=%async_computation.1 | async-start | bytes 1622016 | tf_op jit(solution)/shard_map/all_gather | solution.py:73
  8.6 172.5 %all-gather.13.cloned.1.call-start = ((), (), s32[]{:S(2)}) async-start(), calls=%async_computation.2 | async-start | bytes 1622016 | tf_op jit(solution)/shard_map/all_gather | solution.py:74
  9.4 227.4 %all-gather.9.cloned.1.call-start = ((), (), s32[]{:S(2)}) async-start(), calls=%async_computation | async-start | bytes 1216512 | tf_op jit(solution)/shard_map/all_gather | solution.py:67
  10.0 282.4 %all-gather.17.cloned.1.call-start = ((), (), s32[]{:S(2)}) async-start(), calls=%async_computation.4 | async-start | bytes 1216512 | tf_op jit(solution)/shard_map/all_gather | solution.py:69
  10.5 392.5 %all-gather.19.cloned.1.call-start = ((), (), s32[]{:S(2)}) async-start(), calls=%async_computation.5 | async-start | bytes 1216512 | tf_op jit(solution)/shard_map/all_gather | solution.py:70
  11.1 402.2 %all-gather.21.cloned.1.call-start = ((), (), s32[]{:S(2)}) async-start(), calls=%async_computation.6 | async-start | bytes 4866048 | tf_op jit(solution)/shard_map/all_gather | solution.py:71
  11.9 466.2 %all-gather.23.cloned.1.call-start = ((), (), s32[]{:S(2)}) async-start(), calls=%async_computation.7 | async-start | bytes 4866048 | tf_op jit(solution)/shard_map/all_gather | solution.py:72
  72.6 51.7 %copy-start.45 = (bf16[2,512,768]{2,1,0:T(8,128)(2,1)S(1)}, bf16[2,512,768]{2,1,0:T(8,128)(2,1)}, u32[]{:S(2)}) copy-start(bf16[2,512,768]{2,1,0:T(8,128)(2,1)} %param.25) | copy-start | bytes 4718596
  76.1 105.0 %copy-start.41 = (f32[1024]{0:T(1024)S(1)}, f32[1024]{0:T(1024)}, u32[]{:S(2)}) copy-start(f32[1024]{0:T(1024)} %param.38) | copy-start | bytes 12292
  129.5 107.3 %copy-start.48 = (f32[768]{0:T(1024)S(1)}, f32[768]{0:T(1024)}, u32[]{:S(2)}) copy-start(f32[768]{0:T(1024)} %param.39) | copy-start | bytes 9220
  185.6 51.1 %copy-start.16 = (f32[1024,768]{1,0:T(8,128)}, f32[1024,768]{1,0:T(8,128)S(1)}, u32[]{:S(2)}) copy-start(f32[1024,768]{1,0:T(8,128)S(1)} %fusion.169) | copy-start | bytes 9437188
  247.4 44.9 %copy-start.39 = (f32[768]{0:T(1024)S(1)}, f32[768]{0:T(1024)}, u32[]{:S(2)}) copy-start(f32[768]{0:T(1024)} %param.41) | copy-start | bytes 9220
  251.9 40.5 %copy-start.18 = (f32[1024,768]{1,0:T(8,128)}, f32[1024,768]{1,0:T(8,128)S(1)}, u32[]{:S(2)}) copy-start(f32[1024,768]{1,0:T(8,128)S(1)} %fusion.170) | copy-start | bytes 9437188
  397.3 5.8 copy-start.11
  397.3 5.8 copy-start.25
  479.9 44.2 %copy-start.1 = (f32[1024,768]{1,0:T(8,128)S(1)}, f32[1024,768]{1,0:T(8,128)}, u32[]{:S(2)}) copy-start(f32[1024,768]{1,0:T(8,128)} %copy-done) | copy-start | bytes 9437188
  479.9 44.2 %copy-start.23 = (f32[1024]{0:T(1024)S(1)}, f32[1024]{0:T(1024)}, u32[]{:S(2)}) copy-start(f32[1024]{0:T(1024)} %copy-done.22) | copy-start | bytes 12292
  479.9 44.2 %copy-start.27 = (f32[768]{0:T(1024)S(1)}, f32[768]{0:T(1024)}, u32[]{:S(2)}) copy-start(f32[768]{0:T(1024)} %param.36) | copy-start | bytes 9220
  479.9 44.2 %copy-start.32 = (f32[1024]{0:T(1024)S(1)}, f32[1024]{0:T(1024)}, u32[]{:S(2)}) copy-start(f32[1024]{0:T(1024)} %copy-done.31) | copy-start | bytes 12292
  534.6 67.9 %copy-start.2 = (f32[1024,768]{1,0:T(8,128)S(1)}, f32[1024,768]{1,0:T(8,128)}, u32[]{:S(2)}) copy-start(f32[1024,768]{1,0:T(8,128)} %copy-done) | copy-start | bytes 9437188
  534.6 67.9 %copy-start.24 = (f32[1024]{0:T(1024)S(1)}, f32[1024]{0:T(1024)}, u32[]{:S(2)}) copy-start(f32[1024]{0:T(1024)} %copy-done.22) | copy-start | bytes 12292
  534.6 67.9 %copy-start.28 = (f32[768]{0:T(1024)S(1)}, f32[768]{0:T(1024)}, u32[]{:S(2)}) copy-start(f32[768]{0:T(1024)} %param.36) | copy-start | bytes 9220
  534.6 67.9 %copy-start.35 = (f32[1024]{0:T(1024)S(1)}, f32[1024]{0:T(1024)}, u32[]{:S(2)}) copy-start(f32[1024]{0:T(1024)} %copy-done.34) | copy-start | bytes 12292
  (34 other events, 105.8 us)
Sparse Core Ops, SparseCore 0:
  10.8 56.6 all-gather.14
  70.4 53.8 all-gather.10
  127.2 53.8 all-gather.12
  183.8 52.8 all-gather.8
  239.4 52.8 all-gather.16
  295.0 52.9 all-gather.18
  350.8 62.4 all-gather.20
  416.1 61.9 all-gather.22
where the time goes:
time: 935 us; the launch traced here: 920 us
  matrix products  380 us (41%)
  waiting for transfers between devices  315 us (34%)
  local copies, waits for them, and re-layouts  112 us (12%)
  other arithmetic  52 us (6%)
  blocking collectives  39.8 us (4%)
  between operations  15.6 us (2%)
    dot_general x11, matrix products, dot_plain(): return jnp.dot(left, right, preferred_element_type=jnp.float32)  89.1 us
    dot_general x9, matrix products, dot_trans(): lax.dot_general(left, right, (((1,), (1,)), ((), ())), preferred_element_...  68.1 us
    all_gather x1, waiting for transfers between devices, shards(): lax.all_gather(local_mats[5], ('dp', 'fsdp'), axis=0, tiled=True)  64.7 us
    all_gather x1, waiting for transfers between devices, shards(): lax.all_gather(local_mats[7], ('dp', 'fsdp'), axis=0, tiled=True)  51.7 us
    all_gather x1, waiting for transfers between devices, shards(): lax.all_gather(local_mats[1], ('dp', 'fsdp'), axis=0, tiled=True)  51.6 us
    all_gather x1, waiting for transfers between devices, shards(): lax.all_gather(local_mats[0], ('dp', 'fsdp'), axis=0, tiled=True)  51.1 us
    all_gather x1, waiting for transfers between devices, shards(): lax.all_gather(local_mats[6], ('dp', 'fsdp'), axis=0, tiled=True)  48.2 us
    dot_general x24, matrix products, attend_back(): jnp.einsum('qk,qd->kd', g_scores, q_blk, preferred_element_type=jnp.float32)  43.9 us
  transfers between devices with their start and end apart: 8, of which 7 were waited for; matrix products, arithmetic and copies ran while one was open for 17% of the time, Pallas kernels for 0%

commit v1 on v0

--- a/solution.py
+++ b/solution.py
@@ -2,6 +2,7 @@
 import jax.numpy as jnp
 from jax import lax
 from jax.sharding import PartitionSpec as P
+from jax.lax import axis_index, axis_size, ppermute
 
 D = 768
 H = 12
@@ -60,6 +61,20 @@
     value_d,
     value_b,
 ):
+
+    def tell_kinds(state):
+        dev_axis = ("dp", "fsdp")
+        later = axis_size(dev_axis)
+        plain = axis_index(dev_axis)
+        block_out, known, last = (later, plain, state.shape[0])
+        piece_now, oldest = (state, 1)
+        while oldest < block_out:
+            finding = tuple(((d, (d - oldest) % block_out) for d in range(block_out)))
+            back = ppermute(piece_now, dev_axis, finding)
+            piece_now = jnp.concatenate([piece_now, back], axis=0)
+            oldest = 2 * oldest
+        return jnp.roll(piece_now, known * last, axis=0)
+
     row_count = SEQ_DEV * L
     head_scale = HD ** (-0.5)
     local_mats = (w_query, w_key, w_value, w_out, w_up, w_down, shared_a, shared_b)
@@ -70,7 +85,7 @@
         lax.all_gather(local_mats[3], ("dp", "fsdp"), axis=0, tiled=True),
         lax.all_gather(local_mats[4], ("dp", "fsdp"), axis=0, tiled=True),
         lax.all_gather(local_mats[5], ("dp", "fsdp"), axis=0, tiled=True),
-        lax.all_gather(local_mats[6], ("dp", "fsdp"), axis=0, tiled=True),
+        tell_kinds(local_mats[6]),
         lax.all_gather(local_mats[7], ("dp", "fsdp"), axis=0, tiled=True),
     )
     wq, wk, wv, wo, wu, wd, mat_a, mat_b = full_mats

time: 935 us -> 889 us (0.951)
  waiting for transfers between devices: 315 us -> 236 us
  local copies, waits for them, and re-layouts: 112 us -> 130 us
    all_gather x1, waiting for transfers between devices: 51.6 us -> 0.01 us  [shards(): lax.all_gather(local_mats[1], ('dp', 'fsdp'), axis=0, tiled=True)]
    all_gather x1, waiting for transfers between devices: 48.2 us -> 0.01 us  [shards(): lax.all_gather(local_mats[6], ('dp', 'fsdp'), axis=0, tiled=True)]
    ppermute x0 -> x5, waiting for transfers between devices: none -> 39.7 us  [tell_kinds(): back = ppermute(piece_now, dev_axis, finding)]
    all_gather x1, waiting for transfers between devices: 51.1 us -> 36.9 us  [shards(): lax.all_gather(local_mats[0], ('dp', 'fsdp'), axis=0, tiled=True)]
    all_gather x1, waiting for transfers between devices: 40.4 us -> 51.3 us  [shards(): lax.all_gather(local_mats[2], ('dp', 'fsdp'), axis=0, tiled=True)]
    all_gather x1, waiting for transfers between devices: 51.7 us -> 41.1 us  [shards(): lax.all_gather(local_mats[7], ('dp', 'fsdp'), axis=0, tiled=True)]
    unnamed x105 -> x121, local copies, waits for them, and re-layouts: 10.8 us -> 21.2 us
  transfers between devices with their start and end apart: 8 -> 13, of which waited for: 7 -> 9; matrix products, arithmetic and copies ran while one was open for 17% -> 63% of each run, Pallas kernels for 0% -> 0%
where the time goes in v1:
time: 889 us; the launch traced here: 873 us
  matrix products  388 us (44%)
  waiting for transfers between devices  236 us (27%)
  local copies, waits for them, and re-layouts  130 us (15%)
  other arithmetic  51.2 us (6%)
  blocking collectives  39.8 us (4%)
  between operations  15.9 us (2%)
    dot_general x11, matrix products, dot_plain(): return jnp.dot(left, right, preferred_element_type=jnp.float32)  91.6 us
    dot_general x9, matrix products, dot_trans(): lax.dot_general(left, right, (((1,), (1,)), ((), ())), preferred_element_...  74 us
    all_gather x1, waiting for transfers between devices, shards(): lax.all_gather(local_mats[5], ('dp', 'fsdp'), axis=0, tiled=True)  62.5 us
    all_gather x1, waiting for transfers between devices, shards(): lax.all_gather(local_mats[2], ('dp', 'fsdp'), axis=0, tiled=True)  51.3 us
    dot_general x24, matrix products, attend_back(): jnp.einsum('qk,qd->kd', g_scores, q_blk, preferred_element_type=jnp.float32)  43.7 us
    dot_general x24, matrix products, attend_back(): jnp.dot(g_scores, k_blk, preferred_element_type=jnp.float32) * head_scale  42.7 us
    all_gather x1, waiting for transfers between devices, shards(): lax.all_gather(local_mats[7], ('dp', 'fsdp'), axis=0, tiled=True)  41.1 us
    psum x1, blocking collectives, shards(): lax.psum((grad_qd, grad_qb, grad_vd, grad_vb), ('dp', 'fsdp'))  39.8 us
  transfers between devices with their start and end apart: 13, of which 9 were waited for; matrix products, arithmetic and copies ran while one was open for 63% of the time, Pallas kernels for 0%

profile of v1, /device:TPU:0, one launch (start us, length us, event | category | flops | bytes accessed | tf_op | source)
XLA Modules:
  0.0 873.0 jit_solution(581572281347322326)
XLA Ops:
  11.9 6.5 collective-permute-start
  21.3 7.0 collective-permute-done.1
  36.7 9.3 %collective-permute-done.3 = bf16[192,1024]{1,0:T(8,128)(2,1)S(1)} collective-permute-done((bf16[192,1024]{1,0:T(8,128)(2,1)S(1)}, bf16[192,1024]{1,0:T(8,128)(2,1)S(1)}, u32[]{:S(2)}, u32[]{:S(2)}) %collective-permute-start.3) | collective-permute-done | bytes 393248 | tf_op jit(solution)/shard_map/ppermute | solution.py:73
  50.5 18.1 %collective-permute-done.4 = bf16[384,1024]{1,0:T(8,128)(2,1)S(1)} collective-permute-done((bf16[384,1024]{1,0:T(8,128)(2,1)S(1)}, bf16[384,1024]{1,0:T(8,128)(2,1)S(1)}, u32[]{:S(2)}, u32[]{:S(2)}) %collective-permute-start.4) | collective-permute-done | bytes 786464 | tf_op jit(solution)/shard_map/ppermute | solution.py:73
  73.8 5.3 fusion.190
  87.2 41.1 %all-gather.11.cloned.1.call-done = bf16[1024,768]{1,0:T(8,128)(2,1)} async-done(((bf16[32,768]{1,0:T(8,128)(2,1)}), bf16[1024,768]{1,0:T(8,128)(2,1)}) %all-gather.11.cloned.1.call-update) | async-done | bytes 1572880 | tf_op jit(solution)/shard_map/all_gather | solution.py:89
  132.8 51.3 %all-gather.15.cloned.1.call-done = bf16[768,768]{1,0:T(8,128)(2,1)} async-done(((bf16[24,768]{1,0:T(8,128)(2,1)}), bf16[768,768]{1,0:T(8,128)(2,1)}) %all-gather.15.cloned.1.call-update) | async-done | bytes 1179664 | tf_op jit(solution)/shard_map/all_gather | solution.py:84
  196.6 6.2 fusion.178
  202.7 36.9 %all-gather.9.cloned.1.call-done = bf16[768,768]{1,0:T(8,128)(2,1)} async-done(((bf16[24,768]{1,0:T(8,128)(2,1)}), bf16[768,768]{1,0:T(8,128)(2,1)}) %all-gather.9.cloned.1.call-update) | async-done | bytes 1179664 | tf_op jit(solution)/shard_map/all_gather | solution.py:82
  239.7 5.3 add_convert_fusion.3
  251.3 5.4 copy.61
  258.0 91.2 %while.46 = (s32[]{:T(128)}, bf16[24,512,64]{1,2,0:T(8,128)(2,1)}, f32[24,512]{1,0:T(8,128)}, f32[24,512]{1,0:T(8,128)S(1)}, bf16[24,512,64]{2,1,0:T(8,128)(2,1)...) while((s32[]{:T(128)}, bf16[24,512,64]{1,2,0:T(8,128)(2,1)}, ...), condition=%wide.region_3.4_spmd, body=%wide.region_0.3_spmd.sunk | while | flops 68976640 | bytes 3628133 | solution.py:124
  362.7 62.5 %all-gather.21.cloned.1.call-done = bf16[3072,768]{1,0:T(8,128)(2,1)} async-done(((bf16[96,768]{1,0:T(8,128)(2,1)}), bf16[3072,768]{1,0:T(8,128)(2,1)}) %all-gather.21.cloned.1.call-update) | async-done | bytes 4718608 | tf_op jit(solution)/shard_map/all_gather | solution.py:87
  427.1 44.0 %while.47 = (s32[]{:T(128)}, f32[2,512,768]{2,1,0:T(8,128)}, bf16[2,512,768]{2,1,0:T(8,128)(2,1)}, bf16[768,3072]{1,0:T(8,128)(2,1)}, bf16[3072,768]{1,0:T(8,128)(2,1)}, /*index=5*/s32[]{:T(128)}) while((s32[]{:T(128)}, f32[2,512,768]{2,1,0:T(8,128)}, bf16[2,512,768]{2,1,0:T(8,128)(2,1)}, bf16[768,3072]{1,0:T(8,128)(2,1)}, ...), condition=%wide.region_7.8_spmd, body=%wide.region_6.7_spmd.sunk | while | flops 4934074368 | bytes 11797573 | solution.py:135
  427.1 22.0 %bitcast_dynamic-update-slice_fusion.4 = f32[2,512,768]{2,1,0:T(8,128)} fusion(f32[2,512,768]{2,1,0:T(8,128)} %get-tuple-element.493, s32[]{:T(128)} %get-tuple-element.492, bf16[3072,768]{1,0:T(8,128)(2,1)} %get-tuple-element.502, bf16[768,3072]{1,0:T(8,128)(2,1)} %get-tuple-element.501, bf16[2,512,768]{2,1,0:T(8,128)(2,1)} %get-tuple-element.500), kind=kOutput, calls=%fused_computation.20.clone.1 | convolution fusion | flops 4934074368 | bytes 11797504 | tf_op jit(solution)/shard_map/while/body/eval_jaxpr/dot_general | solution.py:28
  449.1 21.9 %bitcast_dynamic-update-slice_fusion.4 = f32[2,512,768]{2,1,0:T(8,128)} fusion(f32[2,512,768]{2,1,0:T(8,128)} %get-tuple-element.493, s32[]{:T(128)} %get-tuple-element.492, bf16[3072,768]{1,0:T(8,128)(2,1)} %get-tuple-element.502, bf16[768,3072]{1,0:T(8,128)(2,1)} %get-tuple-element.501, bf16[2,512,768]{2,1,0:T(8,128)(2,1)} %get-tuple-element.500), kind=kOutput, calls=%fused_computation.20.clone.1 | convolution fusion | flops 4934074368 | bytes 11797504 | tf_op jit(solution)/shard_map/while/body/eval_jaxpr/dot_general | solution.py:28
  481.6 67.9 %while.48 = (s32[]{:T(128)}, f32[2,512,768]{2,1,0:T(8,128)}, bf16[2,512,768]{2,1,0:T(8,128)(2,1)}, bf16[768,3072]{1,0:T(8,128)(2,1)}, bf16[2,512,768]{2,1,0:T(8,128)(2,1)}, /*index=5*/bf16[3072,768]{1,0:T(8,128)(2,1)}, s32[]{:T(128)}) while((s32[]{:T(128)}, f32[2,512,768]{2,1,0:T(8,128)}, bf16[2,512,768]{2,1,0:T(8,128)(2,1)}, ...), condition=%wide.region_13.14_spmd, body=%wide.region_12.13_spmd.sunk | while | flops 7361003520 | bytes 29886028 | solution.py:162
  484.4 7.9 fusion.271
  492.3 24.7 %bitcast_dynamic-update-slice_fusion.5 = f32[2,512,768]{2,1,0:T(8,128)} fusion(f32[2,512,768]{2,1,0:T(8,128)} %get-tuple-element.512, s32[]{:T(128)} %get-tuple-element.511, bf16[768,3072]{1,0:T(8,128)(2,1)} %get-tuple-element.521, f32[512,3072]{1,0:T(8,128)} %fusion.271, bf16[3072,768]{1,0:T(8,128)(2,1)} %get-tuple-element.523, ...), kind=kOutput, calls=%fused_computation.77.clone.1 | convolution fusion | flops 4945084416 | bytes 18088960 | tf_op jit(solution)/shard_map/while/body/eval_jaxpr/dot_general | solution.py:32
  517.0 7.9 fusion.271
  524.8 24.6 %bitcast_dynamic-update-slice_fusion.5 = f32[2,512,768]{2,1,0:T(8,128)} fusion(f32[2,512,768]{2,1,0:T(8,128)} %get-tuple-element.512, s32[]{:T(128)} %get-tuple-element.511, bf16[768,3072]{1,0:T(8,128)(2,1)} %get-tuple-element.521, f32[512,3072]{1,0:T(8,128)} %fusion.271, bf16[3072,768]{1,0:T(8,128)(2,1)} %get-tuple-element.523, ...), kind=kOutput, calls=%fused_computation.77.clone.1 | convolution fusion | flops 4945084416 | bytes 18088960 | tf_op jit(solution)/shard_map/while/body/eval_jaxpr/dot_general | solution.py:32
  570.6 211.2 %while.49 = (s32[]{:T(128)}, bf16[24,512,64]{1,2,0:T(8,128)(2,1)}, bf16[24,512,64]{1,2,0:T(8,128)(2,1)}, bf16[24,512,64]{1,2,0:T(8,128)(2,1)}, f32[24,512]{1,0:T...) while((s32[]{:T(128)}, bf16[24,512,64]{1,2,0:T(8,128)(2,1)}, ...), condition=%wide.region_18.19_spmd, body=%wide.region_16.18_spmd.sunk | while | flops 170295296 | bytes 8996981 | solution.py:193
  806.3 39.8 %all-reduce = (f32[1024]{0:T(1024)}, f32[768]{0:T(1024)}, f32[1024]{0:T(1024)}, f32[768]{0:T(1024)}, f32[1024]{0:T(1024)S(1)}, /*index=5*/f32[]{:T(128)}) all-reduce(f32[1024]{0:T(1024)S(1)} %get-tuple-element.183, f32[768]{0:T(1024)S(1)} %get-tuple-element.277, ...), channel_id=1, replica_groups=mesh['dp'=8,'fsdp'=4] {'dp','fsdp'}, use_global_device_ids=true, to_apply=%region_20.21 | all-reduce | flops 4609 | bytes 36872 | tf_op jit(solution)/shard_map/psum | solution.py:217
  855.6 5.9 fusion.175
  (543 shorter events, 443.7 us)
Async XLA Ops:
  7.2 62.3 %copy-start.19 = (bf16[24,1024]{1,0:T(8,128)(2,1)S(1)}, bf16[24,1024]{1,0:T(8,128)(2,1)}, u32[]{:S(2)}) copy-start(bf16[24,1024]{1,0:T(8,128)(2,1)} %param.34) | copy-start | bytes 147460
  7.2 71.9 %all-gather.13.cloned.1.call-start = ((), (), s32[]{:S(2)}) async-start(), calls=%async_computation.2 | async-start | bytes 1216512 | tf_op jit(solution)/shard_map/all_gather | solution.py:83
  7.9 120.4 %all-gather.11.cloned.1.call-start = ((), (), s32[]{:S(2)}) async-start(), calls=%async_computation.1 | async-start | bytes 1622016 | tf_op jit(solution)/shard_map/all_gather | solution.py:89
  8.7 175.4 %all-gather.15.cloned.1.call-start = ((), (), s32[]{:S(2)}) async-start(), calls=%async_computation.3 | async-start | bytes 1216512 | tf_op jit(solution)/shard_map/all_gather | solution.py:84
  9.4 230.2 %all-gather.9.cloned.1.call-start = ((), (), s32[]{:S(2)}) async-start(), calls=%async_computation | async-start | bytes 1216512 | tf_op jit(solution)/shard_map/all_gather | solution.py:82
  10.0 345.1 %all-gather.17.cloned.1.call-start = ((), (), s32[]{:S(2)}) async-start(), calls=%async_computation.4 | async-start | bytes 1216512 | tf_op jit(solution)/shard_map/all_gather | solution.py:85
  10.6 352.1 %all-gather.19.cloned.1.call-start = ((), (), s32[]{:S(2)}) async-start(), calls=%async_computation.5 | async-start | bytes 4866048 | tf_op jit(solution)/shard_map/all_gather | solution.py:86
  11.1 414.1 %all-gather.21.cloned.1.call-start = ((), (), s32[]{:S(2)}) async-start(), calls=%async_computation.6 | async-start | bytes 4866048 | tf_op jit(solution)/shard_map/all_gather | solution.py:87
  11.9 843.7 %all-gather.23.cloned.1.call-start = ((), (), s32[]{:S(2)}) async-start(), calls=%async_computation.7 | async-start | bytes 1622016 | tf_op jit(solution)/shard_map/all_gather | solution.py:148
  11.9 8.5 collective-permute-start
  21.3 7.1 collective-permute-start.1
  29.2 3.2 collective-permute-start.2
  33.3 12.8 %collective-permute-start.3 = (bf16[192,1024]{1,0:T(8,128)(2,1)S(1)}, bf16[192,1024]{1,0:T(8,128)(2,1)S(1)}, u32[]{:S(2)}, u32[]{:S(2)}) collective-permute-start(bf16[192,1024]{1,0:T(8,128)(2,1)S(1)} %pad_maximum_fusion), channel_id=1, source_target_pairs={{0,24},{1,25},{2,26},{3,27},{4,28},{5,29},{6,30},{7,31},{8,0},{9,1... | collective-permute-start | bytes 1179656 | tf_op jit(solution)/shard_map/ppermute | solution.py:73
  46.9 21.7 %collective-permute-start.4 = (bf16[384,1024]{1,0:T(8,128)(2,1)S(1)}, bf16[384,1024]{1,0:T(8,128)(2,1)S(1)}, u32[]{:S(2)}, u32[]{:S(2)}) collective-permute-start(bf16[384,1024]{1,0:T(8,128)(2,1)S(1)} %get-tuple-element.260), channel_id=1, source_target_pairs={{0,16},{1,17},{2,18},{3,19},{4,20},{5,21},{6,22},{7,23},{8,24},{9,... | collective-permute-start | bytes 2359304 | tf_op jit(solution)/shard_map/ppermute | solution.py:73
  83.7 44.6 %copy-start.44 = (f32[1024]{0:T(1024)S(1)}, f32[1024]{0:T(1024)}, u32[]{:S(2)}) copy-start(f32[1024]{0:T(1024)} %param.40) | copy-start | bytes 12292
  87.2 96.8 %copy-start.51 = (f32[768]{0:T(1024)S(1)}, f32[768]{0:T(1024)}, u32[]{:S(2)}) copy-start(f32[768]{0:T(1024)} %param.41) | copy-start | bytes 9220
  132.8 51.3 %copy-start.16 = (f32[1024,768]{1,0:T(8,128)}, f32[1024,768]{1,0:T(8,128)S(1)}, u32[]{:S(2)}) copy-start(f32[1024,768]{1,0:T(8,128)S(1)} %fusion.176) | copy-start | bytes 9437188
  427.0 44.0 %copy-start.24 = (f32[1024]{0:T(1024)S(1)}, f32[1024]{0:T(1024)}, u32[]{:S(2)}) copy-start(f32[1024]{0:T(1024)} %copy-done.23) | copy-start | bytes 12292
  427.1 44.1 %copy-start.28 = (f32[768]{0:T(1024)S(1)}, f32[768]{0:T(1024)}, u32[]{:S(2)}) copy-start(f32[768]{0:T(1024)} %param.36) | copy-start | bytes 9220
  427.1 44.1 %copy-start.33 = (f32[1024]{0:T(1024)S(1)}, f32[1024]{0:T(1024)}, u32[]{:S(2)}) copy-start(f32[1024]{0:T(1024)} %copy-done.32) | copy-start | bytes 12292
  481.6 68.0 %copy-start.2 = (f32[1024,768]{1,0:T(8,128)S(1)}, f32[1024,768]{1,0:T(8,128)}, u32[]{:S(2)}) copy-start(f32[1024,768]{1,0:T(8,128)} %copy-done) | copy-start | bytes 9437188
  481.6 68.0 %copy-start.25 = (f32[1024]{0:T(1024)S(1)}, f32[1024]{0:T(1024)}, u32[]{:S(2)}) copy-start(f32[1024]{0:T(1024)} %copy-done.23) | copy-start | bytes 12292
  481.6 68.0 %copy-start.29 = (f32[768]{0:T(1024)S(1)}, f32[768]{0:T(1024)}, u32[]{:S(2)}) copy-start(f32[768]{0:T(1024)} %param.36) | copy-start | bytes 9220
  481.6 68.0 %copy-start.36 = (f32[1024]{0:T(1024)S(1)}, f32[1024]{0:T(1024)}, u32[]{:S(2)}) copy-start(f32[1024]{0:T(1024)} %copy-done.35) | copy-start | bytes 12292
  (42 other events, 295.3 us)
Sparse Core Ops, SparseCore 0:
  10.8 60.5 all-gather.12
  74.3 53.9 all-gather.10
  131.1 52.8 all-gather.14
  186.7 52.8 all-gather.8
  242.3 52.9 all-gather.16
  298.0 62.4 all-gather.18
  363.3 61.8 all-gather.20
  428.1 53.2 all-gather.22
